TPU v7x, 256 devices: a whole 4x4x8 slice. The times are simulated.
256 devices in a mesh: tm: 16 (over x_lo, y, core), strip: 16 (over z, x_hi).
Axes of the slice: x: 4 (x_hi: 2, x_lo: 2; x = x_hi * 2 + x_lo), y: 4, z: 8, core: 2. Of those that a mesh axis runs over, the one named last changes fastest.
Arguments:
- signal: bfloat16 [2, 64, 16384], P(None, 'strip', 'tm'), may hold values from -5 to 5
Outputs:
- spectrum: bfloat16 [2, 256, 64, 16, 1024], P(None, 'strip', None, 'tm')
All inputs are finite; a program needn't handle non-finite values.
Results may differ from a plain program's by a relative error of at most 0.0069.
Values may be sent and summed in bfloat16 or wider, within the bound.
A program may use at most 64 MiB of HBM per device.

v0:
```python
import math

import jax
import jax.numpy as jnp
import numpy as np
from jax import lax
from jax.experimental import pallas as pl
from jax.experimental.pallas import tpu as pltpu
from jax.sharding import PartitionSpec as P

K = 256
J = 64
L = 16384
NB = 16
NA = 16
NW = 64
LB = 1024
NCH = 16
LANES = 128
GW = 8
NZ = 8
KB = 4
QB = 4
TH = 2.0 * math.pi / K
F32 = jnp.float32
BF16 = jnp.bfloat16


ORDER = np.arange(J).reshape(J // 4, 4).T.reshape(J)


def np_bf16(x):
    return np.asarray(x, np.float32).astype(jnp.bfloat16)


def base_table():
    kap = np.arange(-1, NCH + 1)
    r = np.arange(K)
    ang = TH * ((r[:, None] * kap[None, :]) % K)
    c, s = np.cos(ang), np.sin(ang)
    t = np.zeros((4, 2, J, LANES))
    nk = NCH + 2
    c = c.reshape(4, J, nk)[:, ORDER]
    s = s.reshape(4, J, nk)[:, ORDER]
    t[:, 0, :, :nk] = c
    t[:, 1, :, :nk] = s
    t[:, 0, :, nk : 2 * nk] = -s
    t[:, 1, :, nk : 2 * nk] = c
    return np_bf16(t.reshape(4 * LANES, LANES))


def step_tables():
    nk = NCH + 2
    w = np.zeros((NCH // 2, 256, 2, 2, J))
    i = ORDER[:, None]
    j = ORDER[None, :]
    delta = j - i
    ham = (0.54 - 0.46 * np.cos(TH * delta)) / math.sqrt(K) * (delta > 0)
    jj = ORDER
    for k in range(NCH):
        kp, kk = divmod(k, 2)
        gr = ham * np.cos(TH * k * delta)
        gi = ham * np.sin(TH * k * delta)
        w[kp, :J, kk, 0] = gr
        w[kp, :J, kk, 1] = gi
        w[kp, J : 2 * J, kk, 0] = -gi
        w[kp, J : 2 * J, kk, 1] = gr
        for off, coef in ((-1, -0.23), (0, 0.54), (1, -0.23)):
            kap = k + off
            co = coef / math.sqrt(K)
            row = LANES + kap + 1
            w[kp, row, kk, 0] = co * np.cos(TH * kap * jj)
            w[kp, row, kk, 1] = co * np.sin(TH * kap * jj)
            w[kp, row + nk, kk, 0] = -co * np.sin(TH * kap * jj)
            w[kp, row + nk, kk, 1] = co * np.cos(TH * kap * jj)
    return np_bf16(w.reshape(NCH // 2, 256, 256))


def dft_tables():
    group = np.arange(2 * NB * LANES // 2) // 16
    tile, part = group // 8, group % 8
    blk = np.zeros(LB, np.int64)
    low = np.zeros(LB, np.int64)
    for n in range(LB):
        t, q = tile[n], part[n]
        bits = [q % 2, q // 2 % 2]
        low[n] = (t % 2) + 2 * (t // 2 % 2)
        src = (t // 4) * 4 + bits[0] + 2 * bits[1]
        blk[n] = 2 * src + q // 4
    b = blk * J + (np.arange(LB) % 16) * 4 + low
    m = np.arange(LB // 4)
    out = np.zeros((4, 2, LB // 4, 2, LB // 4))
    for r in range(4):
        rows = b[low == r]
        ang = 2.0 * math.pi * ((rows[:, None] * m[None, :]) % LB) / LB
        c, d = np.cos(ang) / math.sqrt(LB), np.sin(ang) / math.sqrt(LB)
        out[r, 0, :, 0] = c
        out[r, 0, :, 1] = -d
        out[r, 1, :, 0] = d
        out[r, 1, :, 1] = c
    return np_bf16(out.reshape(4, LB // 2, LB // 2))


def phase_tables():
    lane = np.arange(LANES)
    left = lane < J
    place = ORDER[lane % J]
    ids = np.arange(16)
    ang = 2.0 * math.pi * ((ids[:, None] * place[None, :]) % 16) / 16
    mod = np.zeros((16, 8, LANES), np.float32)
    mod[:, 0] = np.cos(ang)
    mod[:, 1] = np.where(left, np.sin(ang), -np.sin(ang))
    ang = 2.0 * math.pi * ids[:, None] * place[None, :] / L
    turn = np.zeros((16, 8, LANES), np.float32)
    turn[:, 0] = 0.25 * np.cos(ang)
    turn[:, 1] = 0.25 * np.sin(ang)
    turn[:, 2] = 0.25 * np.where(left, -np.cos(ang), np.cos(ang))
    turn[:, 3] = 0.25 * np.where(left, -np.sin(ang), np.sin(ang))
    ang = np.broadcast_to(2.0 * math.pi * np.arange(K)[:, None] / K, (K, LANES))
    circle = np.stack([np.cos(ang), np.sin(ang)]).astype(np.float32)
    return mod, turn, circle


def pick_table():
    t = np.zeros((2, J, 2, J))
    for lane, j in enumerate(ORDER):
        t[0, j, 0, lane] = 1
        t[1, j, 1, lane] = 1
    return np_bf16(t.reshape(2, J, LANES))


def swap(x):
    return pltpu.roll(x, J, 1)


MESH = pl.DeviceIdType.MESH


def exchange_parts(mine, g, sems):
    (loc, ts, tr_, xs, xr, rs, rr, ls, lr, ds, dr) = sems
    t = lax.axis_index("tm")
    s = lax.axis_index("strip")
    core = t % 2
    q = t // 2
    z = s // 2
    sib = t + 1 - 2 * core
    other = s + 1 - 2 * (s % 2)

    def ring(z_from, e, h, right):
        ref = g.at[2 * z_from + e, core]
        to = (2 * ((z + 1) % NZ) if right else 2 * ((z + NZ - 1) % NZ)) + s % 2
        send, recv = (rs, rr) if right else (ls, lr)
        return pltpu.make_async_remote_copy(
            src_ref=ref,
            dst_ref=ref,
            send_sem=send.at[h, e],
            recv_sem=recv.at[h, e],
            device_id={"strip": to},
            device_id_type=MESH,
        )

    def twin(strip, half, slot):
        ref = g.at[strip, half]
        return pltpu.make_async_remote_copy(
            src_ref=ref,
            dst_ref=ref,
            send_sem=ds.at[slot],
            recv_sem=dr.at[slot],
            device_id={"tm": sib},
            device_id_type=MESH,
        )

    def far(d, half, pos):
        ref = g.at[s, half, pos]
        return pltpu.make_async_remote_copy(
            src_ref=ref,
            dst_ref=ref,
            send_sem=ts.at[d],
            recv_sem=tr_.at[d],
            device_id={"tm": (t + d) % NA},
            device_id_type=MESH,
        )

    def cross(strip):
        ref = g.at[strip, core]
        return pltpu.make_async_remote_copy(
            src_ref=ref,
            dst_ref=ref,
            send_sem=xs,
            recv_sem=xr,
            device_id={"strip": other},
            device_id_type=MESH,
        )

    def slot_of(e, h, right):
        return 1 + (h * 2 + e) * 2 + (0 if right else 1)

    def begin():
        local = pltpu.make_async_copy(mine, g.at[s, core, q], loc)
        local.start()
        barrier = pltpu.get_barrier_semaphore()
        for d in range(1, NA):
            pl.semaphore_signal(barrier, inc=1, device_id={"tm": (t + d) % NA}, device_id_type=MESH)
        for to in (other, 2 * ((z + 1) % NZ) + s % 2, 2 * ((z + NZ - 1) % NZ) + s % 2):
            pl.semaphore_signal(barrier, inc=1, device_id={"strip": to}, device_id_type=MESH)
        pl.semaphore_wait(barrier, NA - 1 + 3)
        local.wait()
        for d in range(1, NA):
            far(d, core, q).start()

    def joined():
        for d in range(1, NA):
            src = (t + NA - d) % NA
            far(d, src % 2, src // 2).wait_recv()
        cross(s).start()
        ring(z, s % 2, 1, True).start()
        ring(z, s % 2, 1, False).start()

    def open_partner():
        cross(other).wait_recv()
        twin(other, core, 0).start()
        ring(z, other % 2, 1, True).start()
        ring(z, other % 2, 1, False).start()
        twin(other, 1 - core, 0).wait_recv()

    def arrive(h, e, right, last=False):
        zf = (z + NZ - h) % NZ if right else (z + h) % NZ
        ring(zf, e, h, right).wait_recv()
        twin(2 * zf + e, core, slot_of(e, h, right)).start()

        if not last:
            if e == (0 if right else 1):
                ring(zf, e, h + 1, right).start()
            else:

                @pl.when(h < 3)
                def _():
                    ring(zf, e, h + 1, right).start()

    def settle(h, e, right):
        zf = (z + NZ - h) % NZ if right else (z + h) % NZ
        twin(2 * zf + e, 1 - core, slot_of(e, h, right)).wait_recv()

    def close():
        for d in range(1, NA):
            far(d, core, q).wait_send()
        cross(s).wait_send()
        twin(other, core, 0).wait_send()
        for right in (True, False):
            for h in range(1, 5):
                for e in range(2):
                    if h == 4 and e != (0 if right else 1):
                        continue
                    zs = (z + NZ - h + 1) % NZ if right else (z + h - 1) % NZ
                    zf = (z + NZ - h) % NZ if right else (z + h) % NZ
                    ring(zs, e, h, right).wait_send()
                    twin(2 * zf + e, core, slot_of(e, h, right)).wait_send()

    return z, begin, joined, open_partner, arrive, settle, close


def body(mine, mod_h, turn_h, circle_h, tr_h, wt_h, sr_h, si_h, g, mod, turn, circle, tr, wt, pce, pse, y32, yb, lhs, va, vb, sr, si, fl, tab, *sems):
    z0, begin, joined, open_partner, arrive, settle, close = exchange_parts(mine, g, sems)
    pairs = ((mod_h.at[lax.axis_index("strip")], mod), (turn_h.at[lax.axis_index("tm")], turn), (circle_h, circle), (tr_h, tr), (wt_h, wt))
    tables = [pltpu.make_async_copy(h, v, tab.at[i]) for i, (h, v) in enumerate(pairs)]
    for c in tables:
        c.start()
    begin()
    left = lax.broadcasted_iota(jnp.int32, (1, LANES), 1) < J
    sign = jnp.where(left, -1.0, 1.0).astype(F32)
    rows_all = NA * NB * GW
    tables[0].wait()
    tables[1].wait()
    mc = mod[0:1, :]
    ms = mod[1:2, :]

    tables[2].wait()
    me = lax.axis_index("tm")
    turns = [jnp.broadcast_to(turn[i : i + 1, :], (GW, LANES)) for i in range(4)]

    def spread(rho, carry):
        at = (me * rho) % K
        ca = jnp.broadcast_to(circle[0, pl.ds(at, 1), :], (GW, LANES))
        sa = jnp.broadcast_to(circle[1, pl.ds(at, 1), :], (GW, LANES))
        dst = pl.ds(pl.multiple_of(rho * GW, GW), GW)
        pce[dst, :] = ca * turns[0] - sa * turns[1]
        pse[dst, :] = sa * turns[2] + ca * turns[3]
        return carry

    lax.fori_loop(0, NA * NB, spread, 0, unroll=8)
    y32[pl.ds(rows_all, 4 * GW), :] = jnp.zeros((4 * GW, LANES), F32)
    yb[pl.ds(rows_all, 4 * GW), :] = jnp.zeros((4 * GW, LANES), BF16)

    joined()
    tables[3].wait()
    tables[4].wait()
    open_partner()

    def flush(z):
        return [pltpu.make_async_copy(v.at[:, z], h.at[:, z], fl.at[z, n]) for n, (v, h) in enumerate(((sr, sr_h), (si, si_h)))]

    def group(i, carry):
        half = (i + 1) // 2
        z = (z0 + NZ + half * (1 - 2 * (i % 2))) % NZ

        @pl.when(i % 2 == 1)
        def _():
            @pl.when(half < 4)
            def _():
                for e in range(2):
                    for right in (True, False):
                        arrive(half, e, right)
                for e in range(2):
                    settle(half, e, True)

            @pl.when(half == 4)
            def _():
                arrive(half, 0, True, True)
                arrive(half, 1, False, True)
                settle(half, 0, True)
                settle(half, 1, False)

        @pl.when((i % 2 == 0) & (i > 0))
        def _():
            for e in range(2):
                settle(half, e, False)

        def load_windows(a, c2):
            for xh in range(2):
                for w in range(4):
                    x = g[2 * z + xh, a % 2, a // 2, w].astype(F32)
                    y = x * mc + swap(x) * ms
                    y32[pl.ds(a * (NB * GW) + xh * 4 + w, NB, stride=GW), :] = y
            return c2

        lax.fori_loop(0, NA, load_windows, 0, unroll=4)

        step = 256
        count = rows_all // step
        for i in range(count + 1):
            if i < count:
                r0 = i * step
                rows = slice(r0, r0 + step)
                y = y32[rows, :]
                yb[rows, :] = y.astype(BF16)
                d = y32[r0 + 4 * GW : r0 + 4 * GW + step, :] - y
                lhs[rows, 0:LANES] = d.astype(BF16)
                y2 = y32[r0 + 2 * GW : r0 + 2 * GW + step, :]
                v = y2 * pce[rows, :] + swap(y2) * pse[rows, :]
                va[rows, :] = v
                vb[rows, :] = swap(v) * sign
            if i > 0:
                r0 = (i - 1) * step
                rows = jnp.concatenate([yb[r0 + q * GW : r0 + q * GW + step, :] for q in range(4)], axis=1)
                base = jnp.dot(rows, tr[...], preferred_element_type=F32)
                lhs[r0 : r0 + step, LANES:] = base.astype(BF16)

        def chan_step(kp, c2):
            w = wt[kp]
            for qb in range(NB // QB):
                cuts = [slice((a * NB + qb * QB) * GW, (a * NB + (qb + 1) * QB) * GW) for a in range(NA)]
                x = jnp.dot(
                    jnp.concatenate([lhs[c, :] for c in cuts], axis=0), w, preferred_element_type=F32
                )
                n = QB * GW
                ta = [None] * 2
                tb = [None] * 2
                for a in range(NA):
                    ua = va[cuts[a], :]
                    ub = vb[cuts[a], :]
                    for kk in range(2):
                        xa = x[a * n : (a + 1) * n, kk * LANES : (kk + 1) * LANES]
                        ta[kk] = xa * ua if a == 0 else ta[kk] + xa * ua
                        tb[kk] = xa * ub if a == 0 else tb[kk] + xa * ub
                for kk in range(2):
                    for t, dst in ((ta[kk], sr), (tb[kk], si)):
                        t = t + swap(t)
                        for h in range(QB // 2):
                            even = t[2 * h * GW : (2 * h + 1) * GW]
                            odd = t[(2 * h + 1) * GW : (2 * h + 2) * GW]
                            lane0 = (qb * QB // 2 + h) * LANES
                            dst[2 * kp + kk, z, :, lane0 : lane0 + LANES] = jnp.where(left, even, odd).astype(BF16)
            return c2

        lax.fori_loop(0, NCH // 2, chan_step, 0, unroll=4)
        for c in flush(z):
            c.start()
        return carry

    lax.fori_loop(0, NW // GW, group, 0)
    for z in range(NZ):
        for c in flush(z):
            c.wait()

    close()


def last_pass(sr, si, tab, out, acc):
    lane = lax.broadcasted_iota(jnp.int32, (1, LANES), 1)
    n = KB * NW

    def regroup(ref):
        t = [ref[:, :, :, i * LANES : (i + 1) * LANES].reshape(n, LANES).astype(F32) for i in range(8)]
        for bit in range(2):
            sh = 16 << bit
            low = (lane // sh) % 2 == 0
            for i in range(8):
                if i >> bit & 1:
                    continue
                p, q = t[i], t[i + (1 << bit)]
                t[i] = jnp.where(low, p, pltpu.roll(q, sh, 1))
                t[i + (1 << bit)] = jnp.where(low, pltpu.roll(p, LANES - sh, 1), q)
        return [x.astype(BF16) for x in t]

    re = regroup(sr)
    im = regroup(si)
    for r in range(4):
        rows = jnp.concatenate([re[r], re[r + 4], im[r], im[r + 4]], axis=1)
        acc[r] = jnp.dot(rows, tab[r], preferred_element_type=F32)
    h = LB // 4
    for c0 in range(0, h, LANES):
        y = [(acc[r, :, c0 : c0 + LANES], acc[r, :, h + c0 : h + c0 + LANES]) for r in range(4)]
        for c in range(2):
            o = 1 - c
            sg = 1.0 if c == 0 else -1.0
            e0 = y[0][c] + y[2][c]
            e1 = y[0][c] - y[2][c]
            o0 = y[1][c] + y[3][c]
            o1 = (y[1][o] - y[3][o]) * sg
            for m1, val in enumerate((e0 + o0, e1 + o1, e0 - o0, e1 - o1)):
                lane0 = m1 * h + c0
                out[c, :, :, lane0 : lane0 + LANES] = val.astype(BF16).reshape(KB, NW, LANES)


def finish(sr, si):
    part = pl.BlockSpec((KB, NW // GW, GW, LB), lambda k: (k, 0, 0, 0))
    return pl.pallas_call(
        last_pass,
        grid=(NCH // KB,),
        out_shape=jax.ShapeDtypeStruct((2, NCH, NW, LB), BF16),
        in_specs=[part, part, pl.BlockSpec((4, LB // 2, LB // 2), lambda k: (0, 0, 0))],
        out_specs=pl.BlockSpec((2, KB, NW, LB), lambda k: (0, k, 0, 0)),
        scratch_shapes=[pltpu.VMEM((4, KB * NW, LB // 2), F32)],
        compiler_params=pltpu.CompilerParams(vmem_limit_bytes=67043328),
    )(sr, si, jnp.asarray(dft_tables()))


def compute(mine):
    hbm = pl.BlockSpec(memory_space=pltpu.HBM)
    dma = pltpu.SemaphoreType.DMA
    rows = NA * NB * GW
    mod, turn, circle = phase_tables()
    strip = jax.ShapeDtypeStruct((NCH, NW // GW, GW, LB), BF16)
    return pl.pallas_call(
        body,
        out_shape=(strip, strip),
        in_specs=[hbm] * 6,
        out_specs=(hbm, hbm),
        scratch_shapes=[
            pltpu.VMEM((2 * NZ, 2, NA // 2, 4, NB, LANES), BF16),
            pltpu.VMEM((8, LANES), F32),
            pltpu.VMEM((8, LANES), F32),
            pltpu.VMEM((2, K, LANES), F32),
            pltpu.VMEM((4 * LANES, LANES), BF16),
            pltpu.VMEM((NCH // 2, 256, 256), BF16),
            pltpu.VMEM((rows, LANES), F32),
            pltpu.VMEM((rows, LANES), F32),
            pltpu.VMEM((rows + 4 * GW, LANES), F32),
            pltpu.VMEM((rows + 4 * GW, LANES), BF16),
            pltpu.VMEM((rows, 256), BF16),
            pltpu.VMEM((rows, LANES), F32),
            pltpu.VMEM((rows, LANES), F32),
            pltpu.VMEM((NCH, NW // GW, GW, LB), BF16),
            pltpu.VMEM((NCH, NW // GW, GW, LB), BF16),
            dma((NZ, 2)),
            dma((5,)),
            dma,
            dma((NA,)),
            dma((NA,)),
            dma,
            dma,
            dma((5, 2)),
            dma((5, 2)),
            dma((5, 2)),
            dma((5, 2)),
            dma((21,)),
            dma((21,)),
        ],
        compiler_params=pltpu.CompilerParams(
            vmem_limit_bytes=67043328, collective_id=0, has_side_effects=True
        ),
    )(mine, jnp.asarray(mod), jnp.asarray(turn), jnp.asarray(circle), jnp.asarray(base_table()), jnp.asarray(step_tables()))


def blocks_of(signal):
    four = signal.shape[1]
    cut = signal.reshape(2, four, NB, J)
    return jnp.einsum("cwbj,cjl->wbl", cut, jnp.asarray(pick_table()), preferred_element_type=F32).astype(BF16)


def per_device(signal):
    sr, si = compute(blocks_of(signal))
    return finish(sr, si).reshape(2, NCH, NW, 1, LB)


def solution(mesh):
    return jax.shard_map(
        per_device,
        mesh=mesh,
        in_specs=(P(None, "strip", "tm"),),
        out_specs=P(None, "strip", None, "tm", None),
        check_vma=False,
    )
```

profile of v0, /device:TPU:1, one launch (start us, length us, event | category | flops | bytes accessed | tf_op | source)
XLA Modules:
  0.0 77.4 jit_solution(6879155012372703860)
XLA Ops:
  0.0 0.8 %reshape.6 = bf16[2,4,16,64]{3,2,1,0:T(8,128)(2,1)S(1)} reshape(bf16[2,4,1024]{2,1,0:T(4,128)(2,1)} %param.8) | data formatting | bytes 32768 | tf_op jit(solution)/shard_map/reshape | solution.py:497
  0.8 1.6 %fusion.1.mine = bf16[4,16,128]{2,1,0:T(8,128)(2,1)} fusion(bf16[2,4,16,64]{3,2,1,0:T(8,128)(2,1)S(1)} %reshape.6, bf16[2,64,128,1]{2,1,0,3:T(8,128)(2,1)} %constant.22), kind=kOutput, calls=%fused_computation.2 | convolution fusion | flops 2105344 | bytes 65536 | tf_op jit(solution)/shard_map/cwbj,cjl->wbl/dot_general | solution.py:498
  2.4 66.5 %shard_map.82 = (bf16[16,8,8,1024]{3,2,1,0:T(8,128)(2,1)}, bf16[16,8,8,1024]{3,2,1,0:T(8,128)(2,1)}) custom-call(bf16[4,16,128]{2,1,0:T(8,128)(2,1)} %fusion.1.mine, f32[16,8,128]{2,1,0:T(8,128)} %constant.15.clone.mod_h, f32[16,8,128]{2,1,0:T(8,128)} %constant.16.clone.turn_h, f32[2,256,128]{2,1,0:T(8,128)} %constant.17.clone.circle_h, ...), custom_call_target="tpu_custom_call" | custom-call | tf_op jit(solution)/shard_map/pallas_call | solution.py:454
  68.9 8.5 %shard_map.83 = bf16[2,16,64,1024]{3,2,1,0:T(8,128)(2,1)} custom-call(bf16[16,8,8,1024]{3,2,1,0:T(8,128)(2,1)} %get-tuple-element.7.sr, bf16[16,8,8,1024]{3,2,1,0:T(8,128)(2,1)} %get-tuple-element.8.si, bf16[4,512,512]{2,1,0:T(8,128)(2,1)} %constant.20.clone.tab), custom_call_target="tpu_custom_call" | custom-call | tf_op jit(solution)/shard_map/pallas_call | solution.py:437
where the time goes:
time: 77.7 us; the launch traced here: 77.4 us
  Pallas kernels  75 us (97%)
  matrix products  1.56 us (2%)
  local copies, waits for them, and re-layouts  0.81 us (1%)
    pallas_call x1, Pallas kernels, compute(): pl.pallas_call(body, out_shape=(strip, strip), in_specs=[hbm] * 6, out_sp...  66.5 us
    pallas_call x1, Pallas kernels, finish(): pl.pallas_call(last_pass, grid=(NCH // KB,), out_shape=jax.ShapeDtypeStru...  8.49 us
    dot_general x1, matrix products, blocks_of(): jnp.einsum('cwbj,cjl->wbl', cut, jnp.asarray(pick_table()), preferred_ele...  1.56 us

commit v1 on v0

--- a/solution.py
+++ b/solution.py
@@ -19,6 +19,7 @@
 LANES = 128
 GW = 8
 NZ = 8
+NQ = 8
 KB = 4
 QB = 4
 TH = 2.0 * math.pi / K
@@ -122,11 +123,12 @@
 
 
 def pick_table():
-    t = np.zeros((2, J, 2, J))
+    t = np.zeros((2, 2, J, 2, 2, J))
     for lane, j in enumerate(ORDER):
-        t[0, j, 0, lane] = 1
-        t[1, j, 1, lane] = 1
-    return np_bf16(t.reshape(2, J, LANES))
+        for c in range(2):
+            for e in range(2):
+                t[c, e, j, e, c, lane] = 1
+    return np_bf16(t.reshape(256, 256))
 
 
 def swap(x):
@@ -136,8 +138,8 @@
 MESH = pl.DeviceIdType.MESH
 
 
-def exchange_parts(mine, g, sems):
-    (loc, ts, tr_, xs, xr, rs, rr, ls, lr, ds, dr) = sems
+def exchange_parts(g, sems):
+    (ts, tr_, xs, xr, rs, rr, ls, lr, ds, dr) = sems
     t = lax.axis_index("tm")
     s = lax.axis_index("strip")
     core = t % 2
@@ -145,17 +147,21 @@
     z = s // 2
     sib = t + 1 - 2 * core
     other = s + 1 - 2 * (s % 2)
+    up = 2 * ((z + 1) % NZ) + s % 2
+    down = 2 * ((z + NZ - 1) % NZ) + s % 2
+
+    def peer(d):
+        return 2 * ((q + d) % NQ) + core
 
     def ring(z_from, e, h, right):
         ref = g.at[2 * z_from + e, core]
-        to = (2 * ((z + 1) % NZ) if right else 2 * ((z + NZ - 1) % NZ)) + s % 2
         send, recv = (rs, rr) if right else (ls, lr)
         return pltpu.make_async_remote_copy(
             src_ref=ref,
             dst_ref=ref,
             send_sem=send.at[h, e],
             recv_sem=recv.at[h, e],
-            device_id={"strip": to},
+            device_id={"strip": up if right else down},
             device_id_type=MESH,
         )
 
@@ -170,58 +176,61 @@
             device_id_type=MESH,
         )
 
-    def far(d, half, pos):
-        ref = g.at[s, half, pos]
+    def near(d, pos):
+        ref = g.at[s, core, pos]
         return pltpu.make_async_remote_copy(
             src_ref=ref,
             dst_ref=ref,
             send_sem=ts.at[d],
             recv_sem=tr_.at[d],
-            device_id={"tm": (t + d) % NA},
+            device_id={"tm": peer(d)},
             device_id_type=MESH,
         )
 
-    def cross(strip):
-        ref = g.at[strip, core]
+    def cross(d, strip, pos):
+        ref = g.at[strip, core, pos]
         return pltpu.make_async_remote_copy(
             src_ref=ref,
             dst_ref=ref,
-            send_sem=xs,
-            recv_sem=xr,
-            device_id={"strip": other},
+            send_sem=xs.at[d],
+            recv_sem=xr.at[d],
+            device_id={"strip": other, "tm": peer(d)},
             device_id_type=MESH,
         )
 
     def slot_of(e, h, right):
-        return 1 + (h * 2 + e) * 2 + (0 if right else 1)
-
-    def begin():
-        local = pltpu.make_async_copy(mine, g.at[s, core, q], loc)
-        local.start()
+        return 2 + (h * 2 + e) * 2 + (0 if right else 1)
+
+    def greet():
         barrier = pltpu.get_barrier_semaphore()
-        for d in range(1, NA):
-            pl.semaphore_signal(barrier, inc=1, device_id={"tm": (t + d) % NA}, device_id_type=MESH)
-        for to in (other, 2 * ((z + 1) % NZ) + s % 2, 2 * ((z + NZ - 1) % NZ) + s % 2):
-            pl.semaphore_signal(barrier, inc=1, device_id={"strip": to}, device_id_type=MESH)
-        pl.semaphore_wait(barrier, NA - 1 + 3)
-        local.wait()
-        for d in range(1, NA):
-            far(d, core, q).start()
+        ids = [{"tm": peer(d)} for d in range(1, NQ)]
+        ids += [{"strip": other, "tm": peer(d)} for d in range(NQ)]
+        ids += [{"tm": sib}, {"strip": up}, {"strip": down}]
+        for to in ids:
+            pl.semaphore_signal(barrier, inc=1, device_id=to, device_id_type=MESH)
+
+    def begin(piece):
+        g[s, core, q] = piece
+        barrier = pltpu.get_barrier_semaphore()
+        pl.semaphore_wait(barrier, 2 * NQ + 2)
+        for d in range(NQ):
+            cross(d, s, q).start()
+            if d:
+                near(d, q).start()
 
     def joined():
-        for d in range(1, NA):
-            src = (t + NA - d) % NA
-            far(d, src % 2, src // 2).wait_recv()
-        cross(s).start()
+        for d in range(1, NQ):
+            near(d, (q + NQ - d) % NQ).wait_recv()
         ring(z, s % 2, 1, True).start()
         ring(z, s % 2, 1, False).start()
-
-    def open_partner():
-        cross(other).wait_recv()
-        twin(other, core, 0).start()
+        twin(s, core, 0).start()
+        for d in range(NQ):
+            cross(d, other, (q + NQ - d) % NQ).wait_recv()
+        twin(other, core, 1).start()
         ring(z, other % 2, 1, True).start()
         ring(z, other % 2, 1, False).start()
-        twin(other, 1 - core, 0).wait_recv()
+        twin(s, 1 - core, 0).wait_recv()
+        twin(other, 1 - core, 1).wait_recv()
 
     def arrive(h, e, right, last=False):
         zf = (z + NZ - h) % NZ if right else (z + h) % NZ
@@ -242,10 +251,12 @@
         twin(2 * zf + e, 1 - core, slot_of(e, h, right)).wait_recv()
 
     def close():
-        for d in range(1, NA):
-            far(d, core, q).wait_send()
-        cross(s).wait_send()
-        twin(other, core, 0).wait_send()
+        for d in range(NQ):
+            cross(d, s, q).wait_send()
+            if d:
+                near(d, q).wait_send()
+        twin(s, core, 0).wait_send()
+        twin(other, core, 1).wait_send()
         for right in (True, False):
             for h in range(1, 5):
                 for e in range(2):
@@ -256,25 +267,38 @@
                     ring(zs, e, h, right).wait_send()
                     twin(2 * zf + e, core, slot_of(e, h, right)).wait_send()
 
-    return z, begin, joined, open_partner, arrive, settle, close
-
-
-def body(mine, mod_h, turn_h, circle_h, tr_h, wt_h, sr_h, si_h, g, mod, turn, circle, tr, wt, pce, pse, y32, yb, lhs, va, vb, sr, si, fl, tab, *sems):
-    z0, begin, joined, open_partner, arrive, settle, close = exchange_parts(mine, g, sems)
-    pairs = ((mod_h.at[lax.axis_index("strip")], mod), (turn_h.at[lax.axis_index("tm")], turn), (circle_h, circle), (tr_h, tr), (wt_h, wt))
+    return z, greet, begin, joined, arrive, settle, close
+
+
+def cut(x, pick):
+    x = x.astype(F32)
+    rows = []
+    for n in range(NB // 2):
+        both = jnp.concatenate([x[c][:, n * LANES : (n + 1) * LANES] for c in range(2)], axis=1)
+        rows += [both, both]
+    out = jnp.dot(jnp.concatenate(rows, axis=0).astype(BF16), pick, preferred_element_type=F32)
+    low = lax.broadcasted_iota(jnp.int32, (4 * NB, LANES), 0) % 8 < 4
+    return jnp.where(low, out[:, :LANES], out[:, LANES:]).astype(BF16)
+
+
+def body(sig_h, pick_h, mod_h, turn_h, circle_h, tr_h, wt_h, sr_h, si_h, g, sig, pick, mod, turn, circle, tr, wt, pce, pse, y32, yb, lhs, va, vb, sr, si, fl, tab, *sems):
+    z0, greet, begin, joined, arrive, settle, close = exchange_parts(g, sems)
+    pairs = ((sig_h, sig), (pick_h, pick), (mod_h.at[lax.axis_index("strip")], mod), (turn_h.at[lax.axis_index("tm")], turn), (circle_h, circle), (tr_h, tr), (wt_h, wt))
     tables = [pltpu.make_async_copy(h, v, tab.at[i]) for i, (h, v) in enumerate(pairs)]
     for c in tables:
         c.start()
-    begin()
+    greet()
+    tables[0].wait()
+    tables[1].wait()
+    begin(cut(sig[...], pick[...]))
     left = lax.broadcasted_iota(jnp.int32, (1, LANES), 1) < J
     sign = jnp.where(left, -1.0, 1.0).astype(F32)
     rows_all = NA * NB * GW
-    tables[0].wait()
-    tables[1].wait()
+    for c in tables[2:5]:
+        c.wait()
     mc = mod[0:1, :]
     ms = mod[1:2, :]
 
-    tables[2].wait()
     me = lax.axis_index("tm")
     turns = [jnp.broadcast_to(turn[i : i + 1, :], (GW, LANES)) for i in range(4)]
 
@@ -291,10 +315,9 @@
     y32[pl.ds(rows_all, 4 * GW), :] = jnp.zeros((4 * GW, LANES), F32)
     yb[pl.ds(rows_all, 4 * GW), :] = jnp.zeros((4 * GW, LANES), BF16)
 
+    for c in tables[5:]:
+        c.wait()
     joined()
-    tables[3].wait()
-    tables[4].wait()
-    open_partner()
 
     def flush(z):
         return [pltpu.make_async_copy(v.at[:, z], h.at[:, z], fl.at[z, n]) for n, (v, h) in enumerate(((sr, sr_h), (si, si_h)))]
@@ -325,12 +348,17 @@
             for e in range(2):
                 settle(half, e, False)
 
+        low = lax.broadcasted_iota(jnp.int32, (1, GW, LANES), 1) < 4
+
         def load_windows(a, c2):
+            y = []
             for xh in range(2):
-                for w in range(4):
-                    x = g[2 * z + xh, a % 2, a // 2, w].astype(F32)
-                    y = x * mc + swap(x) * ms
-                    y32[pl.ds(a * (NB * GW) + xh * 4 + w, NB, stride=GW), :] = y
+                x = g[2 * z + xh, a % 2, a // 2].astype(F32)
+                y.append((x * mc + swap(x) * ms).reshape(NB // 2, GW, LANES))
+            even = jnp.where(low, y[0], pltpu.roll(y[1], 4, 1))
+            odd = jnp.where(low, pltpu.roll(y[0], 4, 1), y[1])
+            both = jnp.stack([even, odd], axis=1).reshape(NB * GW, LANES)
+            y32[pl.ds(pl.multiple_of(a * (NB * GW), NB * GW), NB * GW), :] = both
             return c2
 
         lax.fori_loop(0, NA, load_windows, 0, unroll=4)
@@ -400,7 +428,7 @@
     n = KB * NW
 
     def regroup(ref):
-        t = [ref[:, :, :, i * LANES : (i + 1) * LANES].reshape(n, LANES).astype(F32) for i in range(8)]
+        t = [ref[:, :, :, i * LANES : (i + 1) * LANES].reshape(n, LANES) for i in range(8)]
         for bit in range(2):
             sh = 16 << bit
             low = (lane // sh) % 2 == 0
@@ -410,7 +438,7 @@
                 p, q = t[i], t[i + (1 << bit)]
                 t[i] = jnp.where(low, p, pltpu.roll(q, sh, 1))
                 t[i + (1 << bit)] = jnp.where(low, pltpu.roll(p, LANES - sh, 1), q)
-        return [x.astype(BF16) for x in t]
+        return t
 
     re = regroup(sr)
     im = regroup(si)
@@ -445,7 +473,7 @@
     )(sr, si, jnp.asarray(dft_tables()))
 
 
-def compute(mine):
+def compute(signal):
     hbm = pl.BlockSpec(memory_space=pltpu.HBM)
     dma = pltpu.SemaphoreType.DMA
     rows = NA * NB * GW
@@ -454,10 +482,12 @@
     return pl.pallas_call(
         body,
         out_shape=(strip, strip),
-        in_specs=[hbm] * 6,
+        in_specs=[hbm] * 7,
         out_specs=(hbm, hbm),
         scratch_shapes=[
-            pltpu.VMEM((2 * NZ, 2, NA // 2, 4, NB, LANES), BF16),
+            pltpu.VMEM((2 * NZ, 2, NQ, 4 * NB, LANES), BF16),
+            pltpu.VMEM((2, 4, LB), BF16),
+            pltpu.VMEM((256, 256), BF16),
             pltpu.VMEM((8, LANES), F32),
             pltpu.VMEM((8, LANES), F32),
             pltpu.VMEM((2, K, LANES), F32),
@@ -473,33 +503,26 @@
             pltpu.VMEM((NCH, NW // GW, GW, LB), BF16),
             pltpu.VMEM((NCH, NW // GW, GW, LB), BF16),
             dma((NZ, 2)),
-            dma((5,)),
-            dma,
-            dma((NA,)),
-            dma((NA,)),
-            dma,
-            dma,
+            dma((7,)),
+            dma((NQ,)),
+            dma((NQ,)),
+            dma((NQ,)),
+            dma((NQ,)),
             dma((5, 2)),
             dma((5, 2)),
             dma((5, 2)),
             dma((5, 2)),
-            dma((21,)),
-            dma((21,)),
+            dma((22,)),
+            dma((22,)),
         ],
         compiler_params=pltpu.CompilerParams(
             vmem_limit_bytes=67043328, collective_id=0, has_side_effects=True
         ),
-    )(mine, jnp.asarray(mod), jnp.asarray(turn), jnp.asarray(circle), jnp.asarray(base_table()), jnp.asarray(step_tables()))
-
-
-def blocks_of(signal):
-    four = signal.shape[1]
-    cut = signal.reshape(2, four, NB, J)
-    return jnp.einsum("cwbj,cjl->wbl", cut, jnp.asarray(pick_table()), preferred_element_type=F32).astype(BF16)
+    )(signal, jnp.asarray(pick_table()), jnp.asarray(mod), jnp.asarray(turn), jnp.asarray(circle), jnp.asarray(base_table()), jnp.asarray(step_tables()))
 
 
 def per_device(signal):
-    sr, si = compute(blocks_of(signal))
+    sr, si = compute(signal)
     return finish(sr, si).reshape(2, NCH, NW, 1, LB)
 
 

time: 77.7 us -> 70.5 us (0.907)
  Pallas kernels: 75 us -> 70.3 us
  matrix products: 1.56 us -> 0 us
  local copies, waits for them, and re-layouts: 0.81 us -> 0 us
    pallas_call x1, Pallas kernels: 66.5 us -> 62.1 us  [compute(): pl.pallas_call(body, out_shape=(strip, strip), in_specs=[hbm] * 7, out_sp...]
    dot_general x1 -> x0, matrix products: 1.56 us -> none  [blocks_of(): jnp.einsum('cwbj,cjl->wbl', cut, jnp.asarray(pick_table()), preferred_ele...]
    reshape x1 -> x0, local copies, waits for them, and re-layouts: 0.81 us -> none  [blocks_of(): cut = signal.reshape(2, four, NB, J)]
where the time goes in v1:
time: 70.5 us; the launch traced here: 70.3 us
  Pallas kernels  70.3 us (100%)
    pallas_call x1, Pallas kernels, compute(): pl.pallas_call(body, out_shape=(strip, strip), in_specs=[hbm] * 7, out_sp...  62.1 us
    pallas_call x1, Pallas kernels, finish(): pl.pallas_call(last_pass, grid=(NCH // KB,), out_shape=jax.ShapeDtypeStru...  8.22 us

profile of v1, /device:TPU:1, one launch (start us, length us, event | category | flops | bytes accessed | tf_op | source)
XLA Modules:
  0.0 70.3 jit_solution(15778669577398113755)
XLA Ops:
  0.0 62.1 %shard_map.82 = (bf16[16,8,8,1024]{3,2,1,0:T(8,128)(2,1)}, bf16[16,8,8,1024]{3,2,1,0:T(8,128)(2,1)}) custom-call(bf16[2,4,1024]{2,1,0:T(4,128)(2,1)} %sig_h.1, bf16[256,256]{1,0:T(8,128)(2,1)} %constant.14.clone.pick_h, f32[16,8,128]{2,1,0:T(8,128)} %constant.15.clone.mod_h, f32[16,8,128]{2,1,0:T(8,128)} %constant.16.clone.turn_h, ...), custom_call_target="tpu_custom_call" | custom-call | tf_op jit(solution)/shard_map/pallas_call | solution.py:482
  62.1 8.2 %shard_map.83 = bf16[2,16,64,1024]{3,2,1,0:T(8,128)(2,1)} custom-call(bf16[16,8,8,1024]{3,2,1,0:T(8,128)(2,1)} %get-tuple-element.7.sr, bf16[16,8,8,1024]{3,2,1,0:T(8,128)(2,1)} %get-tuple-element.8.si, bf16[4,512,512]{2,1,0:T(8,128)(2,1)} %constant.20.clone.tab), custom_call_target="tpu_custom_call" | custom-call | tf_op jit(solution)/shard_map/pallas_call | solution.py:465

commit v2 on v1

--- a/solution.py
+++ b/solution.py
@@ -361,9 +361,9 @@
             y32[pl.ds(pl.multiple_of(a * (NB * GW), NB * GW), NB * GW), :] = both
             return c2
 
-        lax.fori_loop(0, NA, load_windows, 0, unroll=4)
-
-        step = 256
+        lax.fori_loop(0, NA, load_windows, 0, unroll=16)
+
+        step = 512
         count = rows_all // step
         for i in range(count + 1):
             if i < count:
@@ -410,7 +410,7 @@
                             dst[2 * kp + kk, z, :, lane0 : lane0 + LANES] = jnp.where(left, even, odd).astype(BF16)
             return c2
 
-        lax.fori_loop(0, NCH // 2, chan_step, 0, unroll=4)
+        lax.fori_loop(0, NCH // 2, chan_step, 0, unroll=8)
         for c in flush(z):
             c.start()
         return carry

time: 70.5 us -> 61.4 us (0.87)
  Pallas kernels: 70.3 us -> 61.2 us
    pallas_call x1, Pallas kernels: 62.1 us -> 53 us  [compute(): pl.pallas_call(body, out_shape=(strip, strip), in_specs=[hbm] * 7, out_sp...]
where the time goes in v2:
time: 61.4 us; the launch traced here: 61.3 us
  Pallas kernels  61.2 us (100%)
    pallas_call x1, Pallas kernels, compute(): pl.pallas_call(body, out_shape=(strip, strip), in_specs=[hbm] * 7, out_sp...  53 us
    pallas_call x1, Pallas kernels, finish(): pl.pallas_call(last_pass, grid=(NCH // KB,), out_shape=jax.ShapeDtypeStru...  8.22 us

profile of v2, /device:TPU:1, one launch (start us, length us, event | category | flops | bytes accessed | tf_op | source)
XLA Modules:
  0.0 61.3 jit_solution(12574243212845800807)
XLA Ops:
  0.0 53.0 %shard_map.82 = (bf16[16,8,8,1024]{3,2,1,0:T(8,128)(2,1)}, bf16[16,8,8,1024]{3,2,1,0:T(8,128)(2,1)}) custom-call(bf16[2,4,1024]{2,1,0:T(4,128)(2,1)} %sig_h.1, bf16[256,256]{1,0:T(8,128)(2,1)} %constant.14.clone.pick_h, f32[16,8,128]{2,1,0:T(8,128)} %constant.15.clone.mod_h, f32[16,8,128]{2,1,0:T(8,128)} %constant.16.clone.turn_h, ...), custom_call_target="tpu_custom_call" | custom-call | tf_op jit(solution)/shard_map/pallas_call | solution.py:482
  53.0 8.2 %shard_map.83 = bf16[2,16,64,1024]{3,2,1,0:T(8,128)(2,1)} custom-call(bf16[16,8,8,1024]{3,2,1,0:T(8,128)(2,1)} %get-tuple-element.7.sr, bf16[16,8,8,1024]{3,2,1,0:T(8,128)(2,1)} %get-tuple-element.8.si, bf16[4,512,512]{2,1,0:T(8,128)(2,1)} %constant.20.clone.tab), custom_call_target="tpu_custom_call" | custom-call | tf_op jit(solution)/shard_map/pallas_call | solution.py:465

commit v3 on v2

--- a/solution.py
+++ b/solution.py
@@ -20,7 +20,9 @@
 GW = 8
 NZ = 8
 NQ = 8
-KB = 4
+KB = 8
+LIM1 = 60600000
+LIM2 = 40 * 2**20
 QB = 4
 TH = 2.0 * math.pi / K
 F32 = jnp.float32
@@ -281,13 +283,15 @@
     return jnp.where(low, out[:, :LANES], out[:, LANES:]).astype(BF16)
 
 
-def body(sig_h, pick_h, mod_h, turn_h, circle_h, tr_h, wt_h, sr_h, si_h, g, sig, pick, mod, turn, circle, tr, wt, pce, pse, y32, yb, lhs, va, vb, sr, si, fl, tab, *sems):
+def body(sig_h, pick_h, mod_h, turn_h, circle_h, tr_h, wt_h, dft_h, sr, si, dft, g, sig, pick, mod, turn, circle, tr, wt, pce, pse, y32, yb, lhs, va, vb, tab, *sems):
     z0, greet, begin, joined, arrive, settle, close = exchange_parts(g, sems)
-    pairs = ((sig_h, sig), (pick_h, pick), (mod_h.at[lax.axis_index("strip")], mod), (turn_h.at[lax.axis_index("tm")], turn), (circle_h, circle), (tr_h, tr), (wt_h, wt))
+    pairs = ((sig_h, sig), (pick_h, pick), (mod_h.at[lax.axis_index("strip")], mod), (turn_h.at[lax.axis_index("tm")], turn), (circle_h, circle), (tr_h, tr), (wt_h, wt), (dft_h, dft))
     tables = [pltpu.make_async_copy(h, v, tab.at[i]) for i, (h, v) in enumerate(pairs)]
-    for c in tables:
+    for c in tables[:2]:
         c.start()
     greet()
+    for c in tables[2:]:
+        c.start()
     tables[0].wait()
     tables[1].wait()
     begin(cut(sig[...], pick[...]))
@@ -315,12 +319,9 @@
     y32[pl.ds(rows_all, 4 * GW), :] = jnp.zeros((4 * GW, LANES), F32)
     yb[pl.ds(rows_all, 4 * GW), :] = jnp.zeros((4 * GW, LANES), BF16)
 
-    for c in tables[5:]:
+    for c in tables[5:7]:
         c.wait()
     joined()
-
-    def flush(z):
-        return [pltpu.make_async_copy(v.at[:, z], h.at[:, z], fl.at[z, n]) for n, (v, h) in enumerate(((sr, sr_h), (si, si_h)))]
 
     def group(i, carry):
         half = (i + 1) // 2
@@ -411,24 +412,21 @@
             return c2
 
         lax.fori_loop(0, NCH // 2, chan_step, 0, unroll=8)
-        for c in flush(z):
-            c.start()
         return carry
 
     lax.fori_loop(0, NW // GW, group, 0)
-    for z in range(NZ):
-        for c in flush(z):
-            c.wait()
-
+
+    tables[7].wait()
     close()
 
 
 def last_pass(sr, si, tab, out, acc):
     lane = lax.broadcasted_iota(jnp.int32, (1, LANES), 1)
     n = KB * NW
+    mine = pl.ds(pl.program_id(0) * KB, KB)
 
     def regroup(ref):
-        t = [ref[:, :, :, i * LANES : (i + 1) * LANES].reshape(n, LANES) for i in range(8)]
+        t = [ref[mine, :, :, i * LANES : (i + 1) * LANES].reshape(n, LANES) for i in range(8)]
         for bit in range(2):
             sh = 16 << bit
             low = (lane // sh) % 2 == 0
@@ -460,30 +458,32 @@
                 out[c, :, :, lane0 : lane0 + LANES] = val.astype(BF16).reshape(KB, NW, LANES)
 
 
-def finish(sr, si):
-    part = pl.BlockSpec((KB, NW // GW, GW, LB), lambda k: (k, 0, 0, 0))
+def finish(sr, si, tab):
+    vm = pl.BlockSpec(memory_space=pltpu.VMEM)
     return pl.pallas_call(
         last_pass,
         grid=(NCH // KB,),
         out_shape=jax.ShapeDtypeStruct((2, NCH, NW, LB), BF16),
-        in_specs=[part, part, pl.BlockSpec((4, LB // 2, LB // 2), lambda k: (0, 0, 0))],
+        in_specs=[vm, vm, vm],
         out_specs=pl.BlockSpec((2, KB, NW, LB), lambda k: (0, k, 0, 0)),
         scratch_shapes=[pltpu.VMEM((4, KB * NW, LB // 2), F32)],
-        compiler_params=pltpu.CompilerParams(vmem_limit_bytes=67043328),
-    )(sr, si, jnp.asarray(dft_tables()))
+        compiler_params=pltpu.CompilerParams(vmem_limit_bytes=LIM2),
+    )(sr, si, tab)
 
 
 def compute(signal):
     hbm = pl.BlockSpec(memory_space=pltpu.HBM)
+    vm = pl.BlockSpec(memory_space=pltpu.VMEM)
     dma = pltpu.SemaphoreType.DMA
     rows = NA * NB * GW
     mod, turn, circle = phase_tables()
-    strip = jax.ShapeDtypeStruct((NCH, NW // GW, GW, LB), BF16)
+    strip = pltpu.VMEM((NCH, NW // GW, GW, LB), BF16)
+    quarter = pltpu.VMEM((4, LB // 2, LB // 2), BF16)
     return pl.pallas_call(
         body,
-        out_shape=(strip, strip),
-        in_specs=[hbm] * 7,
-        out_specs=(hbm, hbm),
+        out_shape=(strip, strip, quarter),
+        in_specs=[hbm] * 8,
+        out_specs=(vm, vm, vm),
         scratch_shapes=[
             pltpu.VMEM((2 * NZ, 2, NQ, 4 * NB, LANES), BF16),
             pltpu.VMEM((2, 4, LB), BF16),
@@ -500,10 +500,7 @@
             pltpu.VMEM((rows, 256), BF16),
             pltpu.VMEM((rows, LANES), F32),
             pltpu.VMEM((rows, LANES), F32),
-            pltpu.VMEM((NCH, NW // GW, GW, LB), BF16),
-            pltpu.VMEM((NCH, NW // GW, GW, LB), BF16),
-            dma((NZ, 2)),
-            dma((7,)),
+            dma((8,)),
             dma((NQ,)),
             dma((NQ,)),
             dma((NQ,)),
@@ -516,14 +513,13 @@
             dma((22,)),
         ],
         compiler_params=pltpu.CompilerParams(
-            vmem_limit_bytes=67043328, collective_id=0, has_side_effects=True
+            vmem_limit_bytes=LIM1, collective_id=0, has_side_effects=True
         ),
-    )(signal, jnp.asarray(pick_table()), jnp.asarray(mod), jnp.asarray(turn), jnp.asarray(circle), jnp.asarray(base_table()), jnp.asarray(step_tables()))
+    )(signal, jnp.asarray(pick_table()), jnp.asarray(mod), jnp.asarray(turn), jnp.asarray(circle), jnp.asarray(base_table()), jnp.asarray(step_tables()), jnp.asarray(dft_tables()))
 
 
 def per_device(signal):
-    sr, si = compute(signal)
-    return finish(sr, si).reshape(2, NCH, NW, 1, LB)
+    return finish(*compute(signal)).reshape(2, NCH, NW, 1, LB)
 
 
 def solution(mesh):

time: 61.4 us -> 57.8 us (0.941)
  Pallas kernels: 61.2 us -> 57.7 us
    pallas_call x1, Pallas kernels: 8.22 us -> 5.67 us  [finish(): pl.pallas_call(last_pass, grid=(NCH // KB,), out_shape=jax.ShapeDtypeStru...]
    pallas_call x1, Pallas kernels: 53 us -> 52 us  [compute(): pl.pallas_call(body, out_shape=(strip, strip, quarter), in_specs=[hbm] *...]
where the time goes in v3:
time: 57.8 us; the launch traced here: 57.7 us
  Pallas kernels  57.7 us (100%)
    pallas_call x1, Pallas kernels, compute(): pl.pallas_call(body, out_shape=(strip, strip, quarter), in_specs=[hbm] *...  52 us
    pallas_call x1, Pallas kernels, finish(): pl.pallas_call(last_pass, grid=(NCH // KB,), out_shape=jax.ShapeDtypeStru...  5.67 us

profile of v3, /device:TPU:1, one launch (start us, length us, event | category | flops | bytes accessed | tf_op | source)
XLA Modules:
  0.0 57.7 jit_solution(6522877243418751644)
XLA Ops:
  0.0 52.0 %shard_map.82 = (bf16[16,8,8,1024]{3,2,1,0:T(8,128)(2,1)S(1)}, bf16[16,8,8,1024]{3,2,1,0:T(8,128)(2,1)S(1)}, bf16[4,512,512]{2,1,0:T(8,128)(2,1)S(1)}) custom-call(bf16[2,4,1024]{2,1,0:T(4,128)(2,1)} %sig_h.1, bf16[256,256]{1,0:T(8,128)(2,1)} %constant.14.clone.pick_h, f32[16,8,128]{2,1,0:T(8,128)} %constant.15.clone.mod_h, ...), custom_call_target="tpu_custom_call" | custom-call | tf_op jit(solution)/shard_map/pallas_call | solution.py:482
  52.0 5.7 %shard_map.83 = bf16[2,16,64,1024]{3,2,1,0:T(8,128)(2,1)} custom-call(bf16[16,8,8,1024]{3,2,1,0:T(8,128)(2,1)S(1)} %get-tuple-element.8.sr, bf16[16,8,8,1024]{3,2,1,0:T(8,128)(2,1)S(1)} %get-tuple-element.9.si, bf16[4,512,512]{2,1,0:T(8,128)(2,1)S(1)} %get-tuple-element.10.tab), custom_call_target="tpu_custom_call" | custom-call | tf_op jit(solution)/shard_map/pallas_call | solution.py:463
